TPU v7x, 256 devices: a whole 4x4x8 slice. The times are simulated.
256 devices in a mesh: freq: 32 (over y, z), pts: 8 (over x, core).
Axes of the slice: x: 4, y: 4, z: 8, core: 2. Of those that a mesh axis runs over, the one named last changes fastest.
Arguments:
- direct: bfloat16 [32, 512, 6144], P('freq', None, 'pts'), may hold values from -6 to 6
- onsets: int32 [32, 6144], P('freq', 'pts'), may hold values from 64 to 511
- left_bases: bfloat16 [128, 24, 24, 2, 8, 256], P('freq', 'pts'), may hold values from -0.4375 to 0.4375
- right_bases: bfloat16 [128, 24, 24, 2, 8, 256], P('freq', 'pts'), may hold values from -0.25 to 0.25
- tile_ranks: int32 [128, 24, 24], P('freq', 'pts'), may hold values from 1 to 8
Outputs:
- plus_field: float32 [32, 512, 6144], P('freq', None, 'pts')
- minus_field: float32 [32, 512, 6144], P('freq', None, 'pts')
All inputs are finite; a program needn't handle non-finite values.
Results may differ from a plain program's by a relative error of at most 0.017.
Values may be sent and summed in bfloat16 or wider, within the bound.
A program may use at most 128 MiB of HBM per device.

v0:
```python
import functools
import math

import jax
import jax.numpy as jnp
import numpy as np
from jax import lax
from jax.experimental import pallas as pl
from jax.experimental.pallas import tpu as pltpu
from jax.sharding import PartitionSpec as P

NB = 256
K = 8
ITERS = 3
NZ = 8
MESH = pl.DeviceIdType.MESH
F32 = jnp.float32
BF16 = jnp.bfloat16


def band_tables(freq_total, sample_total):
    bins = np.arange(freq_total)[:, None] + 1
    moments = np.arange(sample_total)[None, :]
    phases = 2.0 * math.pi / sample_total * (bins * moments % sample_total)
    scaling = 1.0 / math.sqrt(sample_total)
    cosine = np.cos(phases) * scaling
    sine = np.sin(phases) * scaling
    forward = np.stack([cosine, -sine], axis=1).reshape(2 * freq_total, sample_total)
    inverse = np.stack([2.0 * cosine, -2.0 * sine], axis=1).reshape(2 * freq_total, sample_total).T
    return forward, inverse


def row_orders(inner, points):
    order = np.arange(inner * points).reshape(points, inner).T.reshape(-1)
    gather = np.eye(inner * points)[order]
    return gather, gather.T


def dot(left, right, dims=((1,), (0,))):
    return lax.dot_general(left, right, (dims, ((), ())), preferred_element_type=F32)


def spread(index, size):
    return size // 2 + (1 - 2 * lax.rem(index, 2)) * ((index + 1) // 2)


def kernel(
    ny,
    nz,
    npts,
    direct_ref,
    onsets_ref,
    left_ref,
    right_ref,
    ranks_ref,
    fwd_ref,
    inv_ref,
    gather_ref,
    scatter_ref,
    plus_ref,
    minus_ref,
    fields,
    base,
    left_raw,
    right_raw,
    send_f,
    recv_f,
    send_t,
    recv_t,
    send_p,
    recv_p,
    copy_sem,
    base_send,
    base_recv,
    fs_sem,
    fr_sem,
    ts_sem,
    tr_sem,
    ps_sem,
    pr_sem,
    fl_sem,
    tl_sem,
    pl_sem,
):
    nfreq = ny * nz
    tiles = 3
    ntl = npts * tiles
    fh = left_ref.shape[0]
    inner = 2 * fh
    nt = direct_ref.shape[0]
    me_f = lax.axis_index("freq")
    me_p = lax.axis_index("pts")
    my_y = me_f // nz
    my_z = lax.rem(me_f, nz)

    def freq_peer(n):
        dz = spread(n // ny, nz)
        dy = spread(lax.rem(n, ny), ny)
        return lax.rem(my_y + dy, ny) * nz + lax.rem(my_z + dz, nz)

    def pts_peer(n):
        return lax.rem(me_p + spread(n, npts), npts)

    barrier = pltpu.get_barrier_semaphore()

    def greet_f(n, c):
        pl.semaphore_signal(barrier, inc=1, device_id={"freq": freq_peer(n)}, device_id_type=MESH)
        return c

    def greet_p(n, c):
        pl.semaphore_signal(barrier, inc=1, device_id={"pts": pts_peer(n)}, device_id_type=MESH)
        return c

    lax.fori_loop(0, nfreq - 1, greet_f, 0)
    lax.fori_loop(0, npts - 1, greet_p, 0)

    left_copy = pltpu.make_async_copy(left_ref, left_raw, copy_sem.at[0])
    left_copy.start()

    def tile_cols(r):
        return pl.ds(pl.multiple_of(r * NB, NB), NB)

    def band(r, samples):
        spectrum = dot(fwd_ref[...], samples)
        send_f[r] = spectrum.reshape(nfreq, inner, NB).astype(BF16)

    def first_band(r, c):
        samples = direct_ref[:, tile_cols(r)]
        band(r, samples)
        fields[0, :, tile_cols(r)] = jnp.zeros((nt, NB), F32)
        fields[1, :, tile_cols(r)] = samples.astype(F32)
        return c

    lax.fori_loop(0, tiles, first_band, 0)
    pl.semaphore_wait(barrier, nfreq + npts - 2)

    def base_copy(q, source_q):
        return (right_ref.at[:, :, pl.ds(q * tiles, tiles)], right_raw.at[source_q])

    def send_base(n, c):
        q = pts_peer(n)
        src, dst = base_copy(q, me_p)
        pltpu.make_async_remote_copy(
            src, dst, base_send, base_recv, device_id={"pts": q}, device_id_type=MESH
        ).start()
        return c

    def exchange(r, send, recv, send_sem, recv_sem, local_sem):
        def one(n, c):
            d = freq_peer(n)
            pltpu.make_async_remote_copy(
                send.at[r, d],
                recv.at[r, me_f],
                send_sem.at[r],
                recv_sem.at[r],
                device_id={"freq": d},
                device_id_type=MESH,
            ).start()
            return c

        lax.fori_loop(0, nfreq - 1, one, 0)
        pltpu.make_async_copy(send.at[r, me_f], recv.at[r, me_f], local_sem.at[r]).start()

    def await_exchange(r, recv, recv_sem, local_sem):
        others = recv.at[r, pl.ds(0, nfreq - 1)]
        pltpu.make_async_copy(others, others, recv_sem.at[r]).wait()
        own = recv.at[r, me_f]
        pltpu.make_async_copy(own, own, local_sem.at[r]).wait()

    def await_sent(r, send, send_sem):
        others = send.at[r, pl.ds(0, nfreq - 1)]
        pltpu.make_async_copy(others, others, send_sem.at[r]).wait()

    def first_send(r, c):
        exchange(r, send_f, recv_f, fs_sem, fr_sem, fl_sem)
        return c

    lax.fori_loop(0, tiles, first_send, 0)
    lax.fori_loop(0, npts - 1, send_base, 0)
    own_src, own_dst = base_copy(me_p, me_p)
    own_base = pltpu.make_async_copy(own_src, own_dst, copy_sem.at[1])
    own_base.start()

    left_copy.wait()
    rank_row = lax.broadcasted_iota(jnp.int32, (K, NB), 0)

    def stack_left(i, c):
        f, a = i // tiles, lax.rem(i, tiles)
        for comp in range(2):
            rows = []
            for col in range(ntl):
                tile = left_raw[f, a, col, comp].astype(F32)
                rows.append(jnp.where(rank_row < ranks_ref[i, col], tile, 0.0))
            base[1, f, a, comp] = jnp.concatenate(rows, axis=0).astype(BF16)
        return c

    lax.fori_loop(0, fh * tiles, stack_left, 0)
    others = right_raw.at[pl.ds(0, npts - 1)]
    pltpu.make_async_copy(others, others, base_recv).wait()
    own_base.wait()

    def stack_right(i, c):
        f, col = i // tiles, lax.rem(i, tiles)
        for comp in range(2):
            block = right_raw[:, f, :, col, comp].astype(F32)
            base[0, f, col, comp] = block.reshape(ntl * K, NB).astype(BF16)
        return c

    lax.fori_loop(0, fh * tiles, stack_right, 0)

    def half_step(step, carry):
        side = lax.rem(step, 2)
        other = 1 - side

        def coefficients(r, c):
            await_exchange(r, recv_f, fr_sem, fl_sem)
            arrived = recv_f[r].astype(F32).reshape(nfreq * inner, NB).astype(BF16)
            spectrum = dot(gather_ref[...], arrived)
            rows = spectrum.astype(BF16)
            negated = (-spectrum).astype(BF16)
            blank = jnp.zeros((2 * nfreq, NB), BF16)

            @pl.when(step > 0)
            def _():
                sent = send_p.at[0, :, pl.ds(0, ntl - tiles)]
                pltpu.make_async_copy(sent, sent, ps_sem.at[r]).wait()

            for pair in range(fh // 2):
                total = None
                for half in range(2):
                    f = 2 * pair + half
                    lo, mid, hi = (2 * f) * nfreq, (2 * f + 1) * nfreq, (2 * f + 2) * nfreq
                    straight = rows[lo:hi]
                    turned = jnp.concatenate([rows[mid:hi], negated[lo:mid]], axis=0)
                    for comp, part in ((0, straight), (1, turned)):
                        parts = [part, blank] if half == 0 else [blank, part]
                        product = dot(
                            base[side, f, r, comp], jnp.concatenate(parts, axis=0), ((1,), (1,))
                        )
                        total = product if total is None else total + product
                send_p[r, pair] = total.reshape(ntl, K, 4 * nfreq).astype(BF16)

            def one(n, cc):
                q = pts_peer(n)
                pltpu.make_async_remote_copy(
                    send_p.at[r, :, pl.ds(q * tiles, tiles)],
                    recv_p.at[side, me_p * tiles + r],
                    ps_sem.at[r],
                    pr_sem.at[side],
                    device_id={"pts": q},
                    device_id_type=MESH,
                ).start()
                return cc

            lax.fori_loop(0, npts - 1, one, 0)
            own = pltpu.make_async_copy(
                send_p.at[r, :, pl.ds(me_p * tiles, tiles)],
                recv_p.at[side, me_p * tiles + r],
                pl_sem.at[r],
            )
            own.start()
            return c

        lax.fori_loop(0, tiles, coefficients, 0)
        arriving = recv_p.at[side, pl.ds(0, ntl - tiles)]
        pltpu.make_async_copy(arriving, arriving, pr_sem.at[side]).wait()
        for r in range(tiles):
            own = recv_p.at[side, me_p * tiles + r]
            pltpu.make_async_copy(own, own, pl_sem.at[r]).wait()

        def expand(r, c):
            blocks = []
            for pair in range(fh // 2):
                terms = recv_p[side, :, pair, r].astype(F32).reshape(ntl * K, 4 * nfreq)
                terms = jnp.transpose(terms)
                for half in range(2):
                    f = 2 * pair + half
                    real = terms[(2 * half) * nfreq : (2 * half + 1) * nfreq]
                    imag = terms[(2 * half + 1) * nfreq : (2 * half + 2) * nfreq]
                    straight = jnp.concatenate([real, imag], axis=0).astype(BF16)
                    turned = jnp.concatenate([-imag, real], axis=0).astype(BF16)
                    blocks.append(
                        dot(straight, base[other, f, r, 0]) + dot(turned, base[other, f, r, 1])
                    )
            spectrum = jnp.concatenate(blocks, axis=0).astype(BF16)
            ordered = dot(scatter_ref[...], spectrum)

            @pl.when(step > 0)
            def _():
                await_sent(r, send_t, ts_sem)

            send_t[r] = ordered.reshape(nfreq, inner, NB).astype(BF16)
            exchange(r, send_t, recv_t, ts_sem, tr_sem, tl_sem)
            return c

        lax.fori_loop(0, tiles, expand, 0)

        def samples(r, c):
            await_exchange(r, recv_t, tr_sem, tl_sem)
            arrived = recv_t[r].astype(F32).reshape(nfreq * inner, NB).astype(BF16)
            moments = lax.broadcasted_iota(jnp.int32, (nt, NB), 0)
            field = jnp.where(
                moments < onsets_ref[:, tile_cols(r)], dot(inv_ref[...], arrived), 0.0
            )

            @pl.when(step < 2 * ITERS - 1)
            def _():
                await_sent(r, send_f, fs_sem)
                band(r, field.astype(BF16))
                exchange(r, send_f, recv_f, fs_sem, fr_sem, fl_sem)

            fields[side, :, tile_cols(r)] += field
            return c

        lax.fori_loop(0, tiles, samples, 0)
        return carry

    lax.fori_loop(0, 2 * ITERS, half_step, 0)

    minus_out = pltpu.make_async_copy(fields.at[0], minus_ref, copy_sem.at[0])
    plus_out = pltpu.make_async_copy(fields.at[1], plus_ref, copy_sem.at[1])
    minus_out.start()
    plus_out.start()

    def drain(r, c):
        await_sent(r, send_f, fs_sem)
        await_sent(r, send_t, ts_sem)
        sent = send_p.at[0, :, pl.ds(0, ntl - tiles)]
        pltpu.make_async_copy(sent, sent, ps_sem.at[r]).wait()
        return c

    lax.fori_loop(0, tiles, drain, 0)
    sent = right_raw.at[pl.ds(0, npts - 1)]
    pltpu.make_async_copy(sent, sent, base_send).wait()
    minus_out.wait()
    plus_out.wait()


def body(ny, nz, npts, direct, onsets, left_bases, right_bases, tile_ranks):
    nfreq = ny * nz
    fh, tiles, ntl = left_bases.shape[:3]
    _, nt, cells = direct.shape
    freq_total = fh * nfreq
    inner = 2 * fh
    forward, inverse = band_tables(freq_total, nt)
    gather, scatter = row_orders(inner, nfreq)
    tables = [jnp.asarray(t, dtype=BF16) for t in (forward, inverse, gather, scatter)]
    vmem = pl.BlockSpec(memory_space=pltpu.VMEM)
    smem = pl.BlockSpec(memory_space=pltpu.SMEM)
    hbm = pl.BlockSpec(memory_space=pl.ANY)
    dma = pltpu.SemaphoreType.DMA
    slots = pltpu.VMEM((tiles, nfreq, inner, NB), BF16)
    field = jax.ShapeDtypeStruct((nt, cells), F32)
    plus_field, minus_field = pl.pallas_call(
        functools.partial(kernel, ny, nz, npts),
        out_shape=(field, field),
        in_specs=[vmem, vmem, hbm, hbm, smem, vmem, vmem, vmem, vmem],
        out_specs=(hbm, hbm),
        scratch_shapes=[
            pltpu.VMEM((2, nt, cells), F32),
            pltpu.VMEM((2, fh, tiles, 2, ntl * K, NB), BF16),
            pltpu.VMEM((fh, tiles, ntl, 2, K, NB), BF16),
            pltpu.VMEM((npts, fh, tiles, tiles, 2, K, NB), BF16),
            slots,
            slots,
            slots,
            slots,
            pltpu.VMEM((tiles, fh // 2, ntl, K, 4 * nfreq), BF16),
            pltpu.VMEM((2, ntl, fh // 2, tiles, K, 4 * nfreq), BF16),
            dma((2,)),
            dma,
            dma,
            dma((tiles,)),
            dma((tiles,)),
            dma((tiles,)),
            dma((tiles,)),
            dma((tiles,)),
            dma((2,)),
            dma((tiles,)),
            dma((tiles,)),
            dma((tiles,)),
        ],
        compiler_params=pltpu.CompilerParams(
            collective_id=0, has_side_effects=True, vmem_limit_bytes=56 * 1024 * 1024
        ),
    )(
        direct[0],
        onsets,
        left_bases,
        right_bases,
        tile_ranks.reshape(fh * tiles, ntl),
        *tables,
    )
    return plus_field[None], minus_field[None]


def solution(mesh):
    nfreq, npts = mesh.shape["freq"], mesh.shape["pts"]
    nz = NZ if nfreq % NZ == 0 and nfreq > NZ else 2
    return jax.shard_map(
        functools.partial(body, nfreq // nz, nz, npts),
        mesh=mesh,
        in_specs=(
            P("freq", None, "pts"),
            P("freq", "pts"),
            P("freq", "pts", None, None, None, None),
            P("freq", "pts", None, None, None, None),
            P("freq", "pts", None),
        ),
        out_specs=(P("freq", None, "pts"), P("freq", None, "pts")),
        check_vma=False,
    )
```

profile of v0, /device:TPU:1, one launch (start us, length us, event | category | flops | bytes accessed | tf_op | source)
XLA Modules:
  0.0 195.8 jit_solution(16258370385971261573)
XLA Ops:
  0.6 0.7 copy.12
  1.3 0.6 reshape.7.ranks_ref
  1.9 190.0 %shard_map.104 = (f32[512,768]{1,0:T(8,128)}, f32[512,768]{1,0:T(8,128)}) custom-call(bf16[512,768]{1,0:T(8,128)(2,1)} %bitcast.5, s32[1,768]{1,0:T(1,128)} %onsets_ref.1, bf16[4,3,24,2,8,256]{5,4,3,2,1,0:T(8,128)(2,1)} %left_ref.1, bf16[4,3,24,2,8,256]{5,4,3,2,1,0:T(8,128)(2,1)} %right_ref.1, s32[12,24]{1,0:T(8,128)} %reshape.7.ranks_ref, ...), custom_call_target="tpu_custom_call" | custom-call | tf_op jit(solution)/shard_map/pallas_call | solution.py:354
  191.9 0.0 copy-start
  191.9 2.8 %copy.15 = f32[1,512,768]{2,1,0:T(8,128)} copy(f32[1,512,768]{2,1,0:T(8,128)} %bitcast.4) | data formatting | bytes 3145728
  194.7 0.0 copy-done
  194.7 1.1 copy.16
Async XLA Ops:
  191.9 2.8 %copy-start = (f32[512,768]{1,0:T(8,128)S(1)}, f32[512,768]{1,0:T(8,128)}, u32[]{:S(2)}) copy-start(f32[512,768]{1,0:T(8,128)} %get-tuple-element.5) | copy-start | bytes 4718596
where the time goes:
time: 196 us
  Pallas kernels  190 us (97%)
  local copies, waits for them, and re-layouts  5.22 us (3%)
    pallas_call x1, Pallas kernels, body(): pl.pallas_call(functools.partial(kernel, ny, nz, npts), out_shape=(field,...  190 us
    unnamed x5, local copies, waits for them, and re-layouts  4.61 us

commit v1 on v0

v1 whole, which is shorter than its diff:
```python
import functools
import math

import jax
import jax.numpy as jnp
import numpy as np
from jax import lax
from jax.experimental import pallas as pl
from jax.experimental.pallas import tpu as pltpu
from jax.sharding import PartitionSpec as P

NB = 256
K = 8
ITERS = 3
NZ = 8
PAIR = 2
MESH = pl.DeviceIdType.MESH
F32 = jnp.float32
BF16 = jnp.bfloat16


def band_tables(freq_total, sample_total, owners):
    bins = np.arange(freq_total)[:, None] + 1
    moments = np.arange(sample_total)[None, :]
    phases = 2.0 * math.pi / sample_total * (bins * moments % sample_total)
    scaling = 1.0 / math.sqrt(sample_total)
    cosine = np.cos(phases) * scaling
    sine = np.sin(phases) * scaling

    def ordered(table):
        table = table.reshape(owners, freq_total // owners // PAIR, 2 * PAIR, sample_total)
        return np.moveaxis(table, 1, 0).reshape(2 * freq_total, sample_total)

    forward = ordered(np.stack([cosine, -sine], axis=1))
    inverse = ordered(np.stack([2.0 * cosine, -2.0 * sine], axis=1)).T
    return forward, inverse


def row_orders(inner, points):
    order = np.arange(inner * points).reshape(points, inner).T.reshape(-1)
    gather = np.eye(inner * points)[order]
    return gather, gather.T


def dot(left, right, dims=((1,), (0,))):
    return lax.dot_general(left, right, (dims, ((), ())), preferred_element_type=F32)


def spread(index, size):
    return size // 2 + (1 - 2 * (index % 2)) * ((index + 1) // 2)


def kernel(
    ny,
    nz,
    npts,
    direct_hbm,
    onsets_hbm,
    left_ref,
    right_hbm,
    ranks_ref,
    fwd_hbm,
    inv_hbm,
    gather_hbm,
    scatter_hbm,
    fields,
    direct_ref,
    onsets_ref,
    fwd_ref,
    inv_ref,
    gather_ref,
    scatter_ref,
    base,
    left_raw,
    right_ref,
    right_raw,
    send_f,
    recv_f,
    send_t,
    recv_t,
    send_p,
    recv_p,
    load_sem,
    base_send,
    base_recv,
    fs_sem,
    fr_sem,
    ts_sem,
    tr_sem,
    ps_sem,
    pr_sem,
):
    nfreq = ny * nz
    tiles = 3
    ntl = npts * tiles
    fh = left_ref.shape[0]
    pairs = fh // PAIR
    inner = 2 * PAIR
    nt = direct_ref.shape[0]
    me_f = lax.axis_index("freq")
    me_p = lax.axis_index("pts")
    my_y = me_f // nz
    my_z = lax.rem(me_f, nz)

    def freq_peer(n):
        y = lax.rem(my_y + spread(n % ny, ny), ny)
        z = lax.rem(my_z + spread(n // ny, nz), nz)
        return y * nz + z

    def pts_peer(n):
        return lax.rem(me_p + spread(n, npts), npts)

    barrier = pltpu.get_barrier_semaphore()
    for n in range(npts - 1):
        pl.semaphore_signal(barrier, inc=1, device_id={"pts": pts_peer(n)}, device_id_type=MESH)
    for n in range(nfreq - 1):
        pl.semaphore_signal(barrier, inc=1, device_id={"freq": freq_peer(n)}, device_id_type=MESH)

    loads = [
        pltpu.make_async_copy(src, dst, load_sem.at[i])
        for i, (src, dst) in enumerate(
            (
                (direct_hbm.at[0], direct_ref),
                (fwd_hbm, fwd_ref),
                (right_hbm, right_ref),
                (left_ref, left_raw),
                (inv_hbm, inv_ref),
                (gather_hbm, gather_ref),
                (scatter_hbm, scatter_ref),
                (onsets_hbm, onsets_ref),
            )
        )
    ]
    for load in loads:
        load.start()

    def tile_cols(r):
        return pl.ds(pl.multiple_of(r * NB, NB), NB)

    def band(r, samples):
        spectrum = dot(fwd_ref[...], samples)
        send_f[:, r] = spectrum.reshape(pairs, nfreq, inner, NB).astype(BF16)

    loads[0].wait()
    loads[1].wait()

    def first_band(r, c):
        band(r, direct_ref[:, tile_cols(r)])
        return c

    lax.fori_loop(0, tiles, first_band, 0)
    loads[2].wait()
    pl.semaphore_wait(barrier, nfreq + npts - 2)

    def await_all(ref, sem):
        pltpu.make_async_copy(ref, ref, sem).wait()

    def base_part(q, g):
        return right_ref.at[pl.ds(g * PAIR, PAIR), :, pl.ds(q * tiles, tiles)]

    for g in range(pairs):
        for n in range(npts - 1):
            q = pts_peer(n)
            pltpu.make_async_remote_copy(
                base_part(q, g),
                right_raw.at[g, me_p],
                base_send,
                base_recv.at[g],
                device_id={"pts": q},
                device_id_type=MESH,
            ).start()
        pltpu.make_async_copy(base_part(me_p, g), right_raw.at[g, me_p], base_recv.at[g]).start()

    def spectra_out(g, r):
        for n in range(nfreq - 1):
            d = freq_peer(n)
            pltpu.make_async_remote_copy(
                send_f.at[g, r, d],
                recv_f.at[g, r, me_f],
                fs_sem.at[r],
                fr_sem.at[g, r],
                device_id={"freq": d},
                device_id_type=MESH,
            ).start()
        pltpu.make_async_copy(
            send_f.at[g, r, me_f], recv_f.at[g, r, me_f], fr_sem.at[g, r]
        ).start()

    def first_send(i, c):
        spectra_out(i // tiles, lax.rem(i, tiles))
        return c

    lax.fori_loop(0, pairs * tiles, first_send, 0)

    def first_field(r, c):
        fields[0, :, tile_cols(r)] = jnp.zeros((nt, NB), F32)
        fields[1, :, tile_cols(r)] = direct_ref[:, tile_cols(r)].astype(F32)
        return c

    lax.fori_loop(0, tiles, first_field, 0)
    for load in loads[3:]:
        load.wait()

    rank_row = lax.broadcasted_iota(jnp.int32, (K, NB), 0)

    def stack_left(i, c):
        f, a = i // tiles, lax.rem(i, tiles)
        for comp in range(2):
            rows = []
            for col in range(ntl):
                tile = left_raw[f, a, col, comp].astype(F32)
                rows.append(jnp.where(rank_row < ranks_ref[a, f, col], tile, 0.0))
            base[1, f, a, comp] = jnp.concatenate(rows, axis=0).astype(BF16)
        return c

    lax.fori_loop(0, fh * tiles, stack_left, 0)

    def stack_right(g):
        await_all(right_raw.at[g], base_recv.at[g])

        def one(i, c):
            half, col = i // tiles, lax.rem(i, tiles)
            for comp in range(2):
                block = right_raw[g, :, half, :, col, comp].astype(F32)
                base[0, g * PAIR + half, col, comp] = block.reshape(ntl * K, NB).astype(BF16)
            return c

        lax.fori_loop(0, PAIR * tiles, one, 0)

    lanes = inner * nfreq

    def coefficients(step, g, r):
        side = lax.rem(step, 2)

        @pl.when((step == 0) & (r == 0))
        def _():
            stack_right(g)

        await_all(recv_f.at[g, r], fr_sem.at[g, r])
        arrived = recv_f[g, r].astype(F32).reshape(nfreq * inner, NB).astype(BF16)
        spectrum = dot(gather_ref[...], arrived)
        rows = spectrum.astype(BF16)
        negated = (-spectrum).astype(BF16)
        blank = jnp.zeros((lanes // PAIR, NB), BF16)

        @pl.when(step > 0)
        def _():
            await_all(send_p.at[g, 0, pl.ds(0, ntl - tiles)], ps_sem.at[g, r])

        total = None
        for half in range(PAIR):
            lo, mid, hi = (2 * half) * nfreq, (2 * half + 1) * nfreq, (2 * half + 2) * nfreq
            straight = rows[lo:hi]
            turned = jnp.concatenate([rows[mid:hi], negated[lo:mid]], axis=0)
            for comp, part in ((0, straight), (1, turned)):
                parts = [blank] * PAIR
                parts[half] = part
                product = dot(
                    base[side, g * PAIR + half, r, comp],
                    jnp.concatenate(parts, axis=0),
                    ((1,), (1,)),
                )
                total = product if total is None else total + product
        send_p[g, r] = total.reshape(ntl, K, lanes).astype(BF16)

        slot = recv_p.at[side, g, me_p * tiles + r]
        for n in range(npts - 1):
            q = pts_peer(n)
            pltpu.make_async_remote_copy(
                send_p.at[g, r, pl.ds(q * tiles, tiles)],
                slot,
                ps_sem.at[g, r],
                pr_sem.at[side, g],
                device_id={"pts": q},
                device_id_type=MESH,
            ).start()
        pltpu.make_async_copy(
            send_p.at[g, r, pl.ds(me_p * tiles, tiles)], slot, pr_sem.at[side, g]
        ).start()

    def expansion(step, g):
        side = lax.rem(step, 2)
        other = 1 - side
        await_all(recv_p.at[side, g], pr_sem.at[side, g])

        def expand(r, c):
            blocks = []
            terms = recv_p[side, g, :, r].astype(F32).reshape(ntl * K, lanes)
            terms = jnp.transpose(terms)
            for half in range(PAIR):
                lo, mid, hi = (2 * half) * nfreq, (2 * half + 1) * nfreq, (2 * half + 2) * nfreq
                real, imag = terms[lo:mid], terms[mid:hi]
                straight = terms[lo:hi].astype(BF16)
                turned = jnp.concatenate([-imag, real], axis=0).astype(BF16)
                f = g * PAIR + half
                blocks.append(
                    dot(straight, base[other, f, r, 0]) + dot(turned, base[other, f, r, 1])
                )
            ordered = dot(scatter_ref[...], jnp.concatenate(blocks, axis=0).astype(BF16))

            @pl.when(step > 0)
            def _():
                await_all(send_t.at[g, r, pl.ds(0, nfreq - 1)], ts_sem.at[g, r])

            send_t[g, r] = ordered.reshape(nfreq, inner, NB).astype(BF16)
            for n in range(nfreq - 1):
                d = freq_peer(n)
                pltpu.make_async_remote_copy(
                    send_t.at[g, r, d],
                    recv_t.at[r, g, me_f],
                    ts_sem.at[g, r],
                    tr_sem.at[r, g],
                    device_id={"freq": d},
                    device_id_type=MESH,
                ).start()
            pltpu.make_async_copy(
                send_t.at[g, r, me_f], recv_t.at[r, g, me_f], tr_sem.at[r, g]
            ).start()
            return c

        lax.fori_loop(0, tiles, expand, 0)

    def time_work(step):
        side = lax.rem(step, 2)
        last = 2 * ITERS - 1

        def samples(r, c):
            for g in range(pairs):
                await_all(recv_t.at[r, g], tr_sem.at[r, g])
            arrived = recv_t[r].astype(F32).reshape(pairs * nfreq * inner, NB).astype(BF16)
            moments = lax.broadcasted_iota(jnp.int32, (nt, NB), 0)
            field = jnp.where(
                moments < onsets_ref[:, tile_cols(r)], dot(inv_ref[...], arrived), 0.0
            )

            @pl.when(step < last)
            def _():
                await_all(send_f.at[:, r, pl.ds(0, nfreq - 1)], fs_sem.at[r])
                band(r, field.astype(BF16))
                spectra_out(0, r)

            fields[side, :, tile_cols(r)] += field
            return c

        lax.fori_loop(0, tiles, samples, 0)

        @pl.when(step < last)
        def _():
            def one(i, c):
                spectra_out(1 + i // tiles, lax.rem(i, tiles))
                return c

            lax.fori_loop(0, (pairs - 1) * tiles, one, 0)

    def half_step(step, carry):
        count = 3 + 3 * jnp.minimum(step, 1)

        def pair_work(g, c):
            def one(i, cc):
                coefficients(step, i // tiles, lax.rem(i, tiles))
                return cc

            lax.fori_loop(g * count, count + g * (pairs * tiles - count), one, 0)
            expansion(step, g)
            return c

        lax.fori_loop(0, pairs, pair_work, 0)
        time_work(step)
        return carry

    lax.fori_loop(0, 2 * ITERS, half_step, 0)

    def drain(r, c):
        await_all(send_f.at[:, r, pl.ds(0, nfreq - 1)], fs_sem.at[r])
        for g in range(pairs):
            await_all(send_t.at[g, r, pl.ds(0, nfreq - 1)], ts_sem.at[g, r])
            await_all(send_p.at[g, 0, pl.ds(0, ntl - tiles)], ps_sem.at[g, r])
        return c

    lax.fori_loop(0, tiles, drain, 0)
    await_all(right_raw.at[:, pl.ds(0, npts - 1)], base_send)


def body(ny, nz, npts, direct, onsets, left_bases, right_bases, tile_ranks):
    nfreq = ny * nz
    fh, tiles, ntl = left_bases.shape[:3]
    _, nt, cells = direct.shape
    pairs = fh // PAIR
    inner = 2 * PAIR
    forward, inverse = band_tables(fh * nfreq, nt, nfreq)
    gather, scatter = row_orders(inner, nfreq)
    tables = [jnp.asarray(t, dtype=BF16) for t in (forward, inverse, gather, scatter)]
    smem = pl.BlockSpec(memory_space=pltpu.SMEM)
    hbm = pl.BlockSpec(memory_space=pl.ANY)
    dma = pltpu.SemaphoreType.DMA

    def in_hbm(array):
        return pltpu.with_memory_space_constraint(array, pltpu.HBM)

    fields = pl.pallas_call(
        functools.partial(kernel, ny, nz, npts),
        out_shape=jax.ShapeDtypeStruct((2, nt, cells), F32),
        in_specs=[hbm, hbm, hbm, hbm, smem, hbm, hbm, hbm, hbm],
        out_specs=pl.BlockSpec(memory_space=pltpu.VMEM),
        scratch_shapes=[
            pltpu.VMEM((nt, cells), BF16),
            pltpu.VMEM((1, cells), jnp.int32),
            *[pltpu.VMEM(t.shape, BF16) for t in tables],
            pltpu.VMEM((2, fh, tiles, 2, ntl * K, NB), BF16),
            pltpu.VMEM((fh, tiles, ntl, 2, K, NB), BF16),
            pltpu.VMEM((fh, tiles, ntl, 2, K, NB), BF16),
            pltpu.VMEM((pairs, npts, PAIR, tiles, tiles, 2, K, NB), BF16),
            pltpu.VMEM((pairs, tiles, nfreq, inner, NB), BF16),
            pltpu.VMEM((pairs, tiles, nfreq, inner, NB), BF16),
            pltpu.VMEM((pairs, tiles, nfreq, inner, NB), BF16),
            pltpu.VMEM((tiles, pairs, nfreq, inner, NB), BF16),
            pltpu.VMEM((pairs, tiles, ntl, K, inner * nfreq), BF16),
            pltpu.VMEM((2, pairs, ntl, tiles, K, inner * nfreq), BF16),
            dma((8,)),
            dma,
            dma((pairs,)),
            dma((tiles,)),
            dma((pairs, tiles)),
            dma((pairs, tiles)),
            dma((tiles, pairs)),
            dma((pairs, tiles)),
            dma((2, pairs)),
        ],
        compiler_params=pltpu.CompilerParams(
            collective_id=0, has_side_effects=True, vmem_limit_bytes=32 * 1024 * 1024
        ),
    )(
        in_hbm(direct),
        in_hbm(onsets),
        in_hbm(left_bases),
        in_hbm(right_bases),
        jnp.transpose(tile_ranks, (1, 0, 2)),
        *[in_hbm(t) for t in tables],
    )
    return fields[1:], fields[:1]


def solution(mesh):
    nfreq, npts = mesh.shape["freq"], mesh.shape["pts"]
    nz = NZ if nfreq > NZ else 4
    return jax.shard_map(
        functools.partial(body, nfreq // nz, nz, npts),
        mesh=mesh,
        in_specs=(
            P("freq", None, "pts"),
            P("freq", "pts"),
            P("freq", "pts", None, None, None, None),
            P("freq", "pts", None, None, None, None),
            P("freq", "pts", None),
        ),
        out_specs=(P("freq", None, "pts"), P("freq", None, "pts")),
        check_vma=False,
    )
```

time: 196 us -> 180 us (0.918)
  Pallas kernels: 190 us -> 176 us
  local copies, waits for them, and re-layouts: 5.22 us -> 2.55 us
    pallas_call x1, Pallas kernels: 190 us -> 176 us  [body(): pl.pallas_call(functools.partial(kernel, ny, nz, npts), out_shape=jax.Sha...]
    unnamed x5 -> x2, local copies, waits for them, and re-layouts: 4.61 us -> 0.68 us
where the time goes in v1:
time: 180 us
  Pallas kernels  176 us (98%)
  local copies, waits for them, and re-layouts  2.55 us (1%)
    pallas_call x1, Pallas kernels, body(): pl.pallas_call(functools.partial(kernel, ny, nz, npts), out_shape=jax.Sha...  176 us

profile of v1, /device:TPU:1, one launch (start us, length us, event | category | flops | bytes accessed | tf_op | source)
XLA Modules:
  0.0 179.6 jit_solution(15833708522919353045)
XLA Ops:
  0.6 0.0 copy-start
  0.6 0.7 copy-done
  1.3 176.4 %shard_map.104 = f32[2,512,768]{2,1,0:T(8,128)S(1)} custom-call(bf16[1,512,768]{2,1,0:T(8,128)(2,1)} %direct_hbm.1, s32[1,768]{1,0:T(1,128)} %onsets_hbm.1, bf16[4,3,24,2,8,256]{5,4,3,2,1,0:T(8,128)(2,1)} %left_ref.1, bf16[4,3,24,2,8,256]{5,4,3,2,1,0:T(8,128)(2,1)} %right_hbm.1, s32[3,4,24]{2,1,0:T(4,128)S(1)} %bitcast.1, ...), custom_call_target="tpu_custom_call" | custom-call | tf_op jit(solution)/shard_map/pallas_call | solution.py:400
  177.8 1.9 %fusion = (f32[1,512,768]{2,1,0:T(8,128)}, f32[1,512,768]{2,1,0:T(8,128)}) fusion(f32[2,512,768]{2,1,0:T(8,128)S(1)} %shard_map.104), kind=kLoop, calls=%fused_computation | loop fusion | bytes 6291456 | tf_op jit(solution)/shard_map/slice | solution.py:440
Async XLA Ops:
  0.6 0.7 copy-start

commit v2 on v1

--- a/solution.py
+++ b/solution.py
@@ -57,8 +57,8 @@
     direct_hbm,
     onsets_hbm,
     left_ref,
-    right_hbm,
-    ranks_ref,
+    right_ref,
+    ranks_hbm,
     fwd_hbm,
     inv_hbm,
     gather_hbm,
@@ -66,13 +66,13 @@
     fields,
     direct_ref,
     onsets_ref,
+    ranks_ref,
     fwd_ref,
     inv_ref,
     gather_ref,
     scatter_ref,
     base,
     left_raw,
-    right_ref,
     right_raw,
     send_f,
     recv_f,
@@ -102,10 +102,12 @@
     my_y = me_f // nz
     my_z = lax.rem(me_f, nz)
 
+    offsets = [(dy, dz) for dz in range(nz) for dy in range(ny)]
+    offsets.sort(key=lambda o: (-min(o[0], ny - o[0]) - min(o[1], nz - o[1]), o[0], o[1]))
+
     def freq_peer(n):
-        y = lax.rem(my_y + spread(n % ny, ny), ny)
-        z = lax.rem(my_z + spread(n // ny, nz), nz)
-        return y * nz + z
+        dy, dz = offsets[n]
+        return lax.rem(my_y + dy, ny) * nz + lax.rem(my_z + dz, nz)
 
     def pts_peer(n):
         return lax.rem(me_p + spread(n, npts), npts)
@@ -122,12 +124,12 @@
             (
                 (direct_hbm.at[0], direct_ref),
                 (fwd_hbm, fwd_ref),
-                (right_hbm, right_ref),
                 (left_ref, left_raw),
                 (inv_hbm, inv_ref),
                 (gather_hbm, gather_ref),
                 (scatter_hbm, scatter_ref),
                 (onsets_hbm, onsets_ref),
+                (ranks_hbm, ranks_ref),
             )
         )
     ]
@@ -141,35 +143,40 @@
         spectrum = dot(fwd_ref[...], samples)
         send_f[:, r] = spectrum.reshape(pairs, nfreq, inner, NB).astype(BF16)
 
-    loads[0].wait()
-    loads[1].wait()
-
-    def first_band(r, c):
-        band(r, direct_ref[:, tile_cols(r)])
-        return c
-
-    lax.fori_loop(0, tiles, first_band, 0)
-    loads[2].wait()
     pl.semaphore_wait(barrier, nfreq + npts - 2)
 
     def await_all(ref, sem):
         pltpu.make_async_copy(ref, ref, sem).wait()
 
-    def base_part(q, g):
-        return right_ref.at[pl.ds(g * PAIR, PAIR), :, pl.ds(q * tiles, tiles)]
-
-    for g in range(pairs):
+    def base_part(q, g, r):
+        return right_ref.at[pl.ds(g * PAIR, PAIR), :, pl.ds(q * tiles + r, 1)]
+
+    def base_out(i, c):
+        g, r = i // tiles, lax.rem(i, tiles)
         for n in range(npts - 1):
             q = pts_peer(n)
             pltpu.make_async_remote_copy(
-                base_part(q, g),
-                right_raw.at[g, me_p],
+                base_part(q, g, r),
+                right_raw.at[g, r, me_p],
                 base_send,
-                base_recv.at[g],
+                base_recv.at[g, r],
                 device_id={"pts": q},
                 device_id_type=MESH,
             ).start()
-        pltpu.make_async_copy(base_part(me_p, g), right_raw.at[g, me_p], base_recv.at[g]).start()
+        pltpu.make_async_copy(
+            base_part(me_p, g, r), right_raw.at[g, r, me_p], base_recv.at[g, r]
+        ).start()
+        return c
+
+    lax.fori_loop(0, pairs * tiles, base_out, 0)
+    loads[0].wait()
+    loads[1].wait()
+
+    def first_band(r, c):
+        band(r, direct_ref[:, tile_cols(r)])
+        return c
+
+    lax.fori_loop(0, tiles, first_band, 0)
 
     def spectra_out(g, r):
         for n in range(nfreq - 1):
@@ -198,7 +205,7 @@
         return c
 
     lax.fori_loop(0, tiles, first_field, 0)
-    for load in loads[3:]:
+    for load in loads[2:]:
         load.wait()
 
     rank_row = lax.broadcasted_iota(jnp.int32, (K, NB), 0)
@@ -215,26 +222,21 @@
 
     lax.fori_loop(0, fh * tiles, stack_left, 0)
 
-    def stack_right(g):
-        await_all(right_raw.at[g], base_recv.at[g])
-
-        def one(i, c):
-            half, col = i // tiles, lax.rem(i, tiles)
+    def stack_right(g, r):
+        await_all(right_raw.at[g, r], base_recv.at[g, r])
+        for half in range(PAIR):
             for comp in range(2):
-                block = right_raw[g, :, half, :, col, comp].astype(F32)
-                base[0, g * PAIR + half, col, comp] = block.reshape(ntl * K, NB).astype(BF16)
-            return c
-
-        lax.fori_loop(0, PAIR * tiles, one, 0)
+                block = right_raw[g, r, :, half, :, 0, comp].astype(F32)
+                base[0, g * PAIR + half, r, comp] = block.reshape(ntl * K, NB).astype(BF16)
 
     lanes = inner * nfreq
 
     def coefficients(step, g, r):
         side = lax.rem(step, 2)
 
-        @pl.when((step == 0) & (r == 0))
+        @pl.when(step == 0)
         def _():
-            stack_right(g)
+            stack_right(g, r)
 
         await_all(recv_f.at[g, r], fr_sem.at[g, r])
         arrived = recv_f[g, r].astype(F32).reshape(nfreq * inner, NB).astype(BF16)
@@ -278,6 +280,21 @@
             send_p.at[g, r, pl.ds(me_p * tiles, tiles)], slot, pr_sem.at[side, g]
         ).start()
 
+    def results_out(g, r):
+        for n in range(nfreq - 1):
+            d = freq_peer(n)
+            pltpu.make_async_remote_copy(
+                send_t.at[g, r, d],
+                recv_t.at[r, g, me_f],
+                ts_sem.at[g, r],
+                tr_sem.at[r, g],
+                device_id={"freq": d},
+                device_id_type=MESH,
+            ).start()
+        pltpu.make_async_copy(
+            send_t.at[g, r, me_f], recv_t.at[r, g, me_f], tr_sem.at[r, g]
+        ).start()
+
     def expansion(step, g):
         side = lax.rem(step, 2)
         other = 1 - side
@@ -303,19 +320,15 @@
                 await_all(send_t.at[g, r, pl.ds(0, nfreq - 1)], ts_sem.at[g, r])
 
             send_t[g, r] = ordered.reshape(nfreq, inner, NB).astype(BF16)
-            for n in range(nfreq - 1):
-                d = freq_peer(n)
-                pltpu.make_async_remote_copy(
-                    send_t.at[g, r, d],
-                    recv_t.at[r, g, me_f],
-                    ts_sem.at[g, r],
-                    tr_sem.at[r, g],
-                    device_id={"freq": d},
-                    device_id_type=MESH,
-                ).start()
-            pltpu.make_async_copy(
-                send_t.at[g, r, me_f], recv_t.at[r, g, me_f], tr_sem.at[r, g]
-            ).start()
+
+            @pl.when((g > 0) | (r < tiles - 1))
+            def _():
+                results_out(g, r)
+
+            @pl.when((g == 1) & (r == tiles - 2))
+            def _():
+                results_out(0, tiles - 1)
+
             return c
 
         lax.fori_loop(0, tiles, expand, 0)
@@ -339,6 +352,10 @@
                 band(r, field.astype(BF16))
                 spectra_out(0, r)
 
+            @pl.when((step < last) & (r == tiles - 2))
+            def _():
+                spectra_out(1, 0)
+
             fields[side, :, tile_cols(r)] += field
             return c
 
@@ -346,25 +363,24 @@
 
         @pl.when(step < last)
         def _():
-            def one(i, c):
-                spectra_out(1 + i // tiles, lax.rem(i, tiles))
+            def one(r, c):
+                spectra_out(1, r)
                 return c
 
-            lax.fori_loop(0, (pairs - 1) * tiles, one, 0)
+            lax.fori_loop(1, tiles, one, 0)
 
     def half_step(step, carry):
-        count = 3 + 3 * jnp.minimum(step, 1)
-
-        def pair_work(g, c):
-            def one(i, cc):
-                coefficients(step, i // tiles, lax.rem(i, tiles))
-                return cc
-
-            lax.fori_loop(g * count, count + g * (pairs * tiles - count), one, 0)
+        def one(i, c):
+            order = jnp.where(i == 2, 3, jnp.where(i == 3, 2, i))
+            coefficients(step, order // tiles, lax.rem(order, tiles))
+            return c
+
+        def two(g, c):
             expansion(step, g)
             return c
 
-        lax.fori_loop(0, pairs, pair_work, 0)
+        lax.fori_loop(0, pairs * tiles, one, 0)
+        lax.fori_loop(0, pairs, two, 0)
         time_work(step)
         return carry
 
@@ -378,7 +394,7 @@
         return c
 
     lax.fori_loop(0, tiles, drain, 0)
-    await_all(right_raw.at[:, pl.ds(0, npts - 1)], base_send)
+    await_all(right_raw.at[:, :, pl.ds(0, npts - 1)], base_send)
 
 
 def body(ny, nz, npts, direct, onsets, left_bases, right_bases, tile_ranks):
@@ -390,7 +406,6 @@
     forward, inverse = band_tables(fh * nfreq, nt, nfreq)
     gather, scatter = row_orders(inner, nfreq)
     tables = [jnp.asarray(t, dtype=BF16) for t in (forward, inverse, gather, scatter)]
-    smem = pl.BlockSpec(memory_space=pltpu.SMEM)
     hbm = pl.BlockSpec(memory_space=pl.ANY)
     dma = pltpu.SemaphoreType.DMA
 
@@ -400,16 +415,16 @@
     fields = pl.pallas_call(
         functools.partial(kernel, ny, nz, npts),
         out_shape=jax.ShapeDtypeStruct((2, nt, cells), F32),
-        in_specs=[hbm, hbm, hbm, hbm, smem, hbm, hbm, hbm, hbm],
+        in_specs=[hbm] * 9,
         out_specs=pl.BlockSpec(memory_space=pltpu.VMEM),
         scratch_shapes=[
             pltpu.VMEM((nt, cells), BF16),
             pltpu.VMEM((1, cells), jnp.int32),
+            pltpu.SMEM((tiles, fh, ntl), jnp.int32),
             *[pltpu.VMEM(t.shape, BF16) for t in tables],
             pltpu.VMEM((2, fh, tiles, 2, ntl * K, NB), BF16),
             pltpu.VMEM((fh, tiles, ntl, 2, K, NB), BF16),
-            pltpu.VMEM((fh, tiles, ntl, 2, K, NB), BF16),
-            pltpu.VMEM((pairs, npts, PAIR, tiles, tiles, 2, K, NB), BF16),
+            pltpu.VMEM((pairs, tiles, npts, PAIR, tiles, 1, 2, K, NB), BF16),
             pltpu.VMEM((pairs, tiles, nfreq, inner, NB), BF16),
             pltpu.VMEM((pairs, tiles, nfreq, inner, NB), BF16),
             pltpu.VMEM((pairs, tiles, nfreq, inner, NB), BF16),
@@ -418,7 +433,7 @@
             pltpu.VMEM((2, pairs, ntl, tiles, K, inner * nfreq), BF16),
             dma((8,)),
             dma,
-            dma((pairs,)),
+            dma((pairs, tiles)),
             dma((tiles,)),
             dma((pairs, tiles)),
             dma((pairs, tiles)),
@@ -434,7 +449,7 @@
         in_hbm(onsets),
         in_hbm(left_bases),
         in_hbm(right_bases),
-        jnp.transpose(tile_ranks, (1, 0, 2)),
+        in_hbm(jnp.transpose(tile_ranks, (1, 0, 2))),
         *[in_hbm(t) for t in tables],
     )
     return fields[1:], fields[:1]

time: 180 us -> 175 us (0.972)
  Pallas kernels: 176 us -> 173 us
    pallas_call x1, Pallas kernels: 176 us -> 173 us  [body(): pl.pallas_call(functools.partial(kernel, ny, nz, npts), out_shape=jax.Sha...]
where the time goes in v2:
time: 175 us
  Pallas kernels  173 us (99%)
  local copies, waits for them, and re-layouts  1.86 us (1%)
    pallas_call x1, Pallas kernels, body(): pl.pallas_call(functools.partial(kernel, ny, nz, npts), out_shape=jax.Sha...  173 us

profile of v2, /device:TPU:1, one launch (start us, length us, event | category | flops | bytes accessed | tf_op | source)
XLA Modules:
  0.0 175.1 jit_solution(6883549214640433416)
XLA Ops:
  0.6 172.6 %shard_map.104 = f32[2,512,768]{2,1,0:T(8,128)S(1)} custom-call(bf16[1,512,768]{2,1,0:T(8,128)(2,1)} %direct_hbm.1, s32[1,768]{1,0:T(1,128)} %onsets_hbm.1, bf16[4,3,24,2,8,256]{5,4,3,2,1,0:T(8,128)(2,1)} %left_ref.1, bf16[4,3,24,2,8,256]{5,4,3,2,1,0:T(8,128)(2,1)} %right_ref.1, s32[3,4,24]{2,1,0:T(4,128)} %bitcast.1, ...), custom_call_target="tpu_custom_call" | custom-call | tf_op jit(solution)/shard_map/pallas_call | solution.py:415
  173.2 1.9 %fusion = (f32[1,512,768]{2,1,0:T(8,128)}, f32[1,512,768]{2,1,0:T(8,128)}) fusion(f32[2,512,768]{2,1,0:T(8,128)S(1)} %shard_map.104), kind=kLoop, calls=%fused_computation | loop fusion | bytes 6291456 | tf_op jit(solution)/shard_map/slice | solution.py:455

commit v3 on v2

--- a/solution.py
+++ b/solution.py
@@ -34,12 +34,6 @@
     forward = ordered(np.stack([cosine, -sine], axis=1))
     inverse = ordered(np.stack([2.0 * cosine, -2.0 * sine], axis=1)).T
     return forward, inverse
-
-
-def row_orders(inner, points):
-    order = np.arange(inner * points).reshape(points, inner).T.reshape(-1)
-    gather = np.eye(inner * points)[order]
-    return gather, gather.T
 
 
 def dot(left, right, dims=((1,), (0,))):
@@ -61,16 +55,12 @@
     ranks_hbm,
     fwd_hbm,
     inv_hbm,
-    gather_hbm,
-    scatter_hbm,
     fields,
     direct_ref,
     onsets_ref,
     ranks_ref,
     fwd_ref,
     inv_ref,
-    gather_ref,
-    scatter_ref,
     base,
     left_raw,
     right_raw,
@@ -126,8 +116,6 @@
                 (fwd_hbm, fwd_ref),
                 (left_ref, left_raw),
                 (inv_hbm, inv_ref),
-                (gather_hbm, gather_ref),
-                (scatter_hbm, scatter_ref),
                 (onsets_hbm, onsets_ref),
                 (ranks_hbm, ranks_ref),
             )
@@ -139,9 +127,10 @@
     def tile_cols(r):
         return pl.ds(pl.multiple_of(r * NB, NB), NB)
 
-    def band(r, samples):
-        spectrum = dot(fwd_ref[...], samples)
-        send_f[:, r] = spectrum.reshape(pairs, nfreq, inner, NB).astype(BF16)
+    def band(g, r, samples):
+        rows = nfreq * inner
+        spectrum = dot(fwd_ref[g * rows : (g + 1) * rows], samples)
+        send_f[g, r] = spectrum.reshape(nfreq, inner, NB).astype(BF16)
 
     pl.semaphore_wait(barrier, nfreq + npts - 2)
 
@@ -173,7 +162,8 @@
     loads[1].wait()
 
     def first_band(r, c):
-        band(r, direct_ref[:, tile_cols(r)])
+        for g in range(pairs):
+            band(g, r, direct_ref[:, tile_cols(r)])
         return c
 
     lax.fori_loop(0, tiles, first_band, 0)
@@ -231,6 +221,19 @@
 
     lanes = inner * nfreq
 
+    def row_of(width):
+        return lax.broadcasted_iota(jnp.int32, (lanes, width), 0)
+
+    def bin_row(width):
+        return lax.rem(row_of(width), inner) // 2
+
+    def swapped(values, sign):
+        width = values.shape[1]
+        after = pltpu.roll(values, lanes - 1, 0)
+        before = pltpu.roll(values, 1, 0)
+        even = lax.rem(row_of(width), 2) == 0
+        return jnp.where(even, sign * after, -sign * before)
+
     def coefficients(step, g, r):
         side = lax.rem(step, 2)
 
@@ -239,11 +242,8 @@
             stack_right(g, r)
 
         await_all(recv_f.at[g, r], fr_sem.at[g, r])
-        arrived = recv_f[g, r].astype(F32).reshape(nfreq * inner, NB).astype(BF16)
-        spectrum = dot(gather_ref[...], arrived)
-        rows = spectrum.astype(BF16)
-        negated = (-spectrum).astype(BF16)
-        blank = jnp.zeros((lanes // PAIR, NB), BF16)
+        arrived = recv_f[g, r].astype(F32).reshape(lanes, NB)
+        turned = swapped(arrived, 1.0)
 
         @pl.when(step > 0)
         def _():
@@ -251,15 +251,11 @@
 
         total = None
         for half in range(PAIR):
-            lo, mid, hi = (2 * half) * nfreq, (2 * half + 1) * nfreq, (2 * half + 2) * nfreq
-            straight = rows[lo:hi]
-            turned = jnp.concatenate([rows[mid:hi], negated[lo:mid]], axis=0)
-            for comp, part in ((0, straight), (1, turned)):
-                parts = [blank] * PAIR
-                parts[half] = part
+            here = bin_row(NB) == half
+            for comp, part in ((0, arrived), (1, turned)):
                 product = dot(
                     base[side, g * PAIR + half, r, comp],
-                    jnp.concatenate(parts, axis=0),
+                    jnp.where(here, part, 0.0).astype(BF16),
                     ((1,), (1,)),
                 )
                 total = product if total is None else total + product
@@ -301,19 +297,15 @@
         await_all(recv_p.at[side, g], pr_sem.at[side, g])
 
         def expand(r, c):
-            blocks = []
             terms = recv_p[side, g, :, r].astype(F32).reshape(ntl * K, lanes)
             terms = jnp.transpose(terms)
+            turned = swapped(terms, -1.0).astype(BF16)
+            terms = terms.astype(BF16)
+            ordered = None
             for half in range(PAIR):
-                lo, mid, hi = (2 * half) * nfreq, (2 * half + 1) * nfreq, (2 * half + 2) * nfreq
-                real, imag = terms[lo:mid], terms[mid:hi]
-                straight = terms[lo:hi].astype(BF16)
-                turned = jnp.concatenate([-imag, real], axis=0).astype(BF16)
                 f = g * PAIR + half
-                blocks.append(
-                    dot(straight, base[other, f, r, 0]) + dot(turned, base[other, f, r, 1])
-                )
-            ordered = dot(scatter_ref[...], jnp.concatenate(blocks, axis=0).astype(BF16))
+                mine = dot(terms, base[other, f, r, 0]) + dot(turned, base[other, f, r, 1])
+                ordered = mine if half == 0 else jnp.where(bin_row(NB) == half, mine, ordered)
 
             @pl.when(step > 0)
             def _():
@@ -349,8 +341,11 @@
             @pl.when(step < last)
             def _():
                 await_all(send_f.at[:, r, pl.ds(0, nfreq - 1)], fs_sem.at[r])
-                band(r, field.astype(BF16))
+                values = field.astype(BF16)
+                band(0, r, values)
                 spectra_out(0, r)
+                for g in range(1, pairs):
+                    band(g, r, values)
 
             @pl.when((step < last) & (r == tiles - 2))
             def _():
@@ -404,8 +399,7 @@
     pairs = fh // PAIR
     inner = 2 * PAIR
     forward, inverse = band_tables(fh * nfreq, nt, nfreq)
-    gather, scatter = row_orders(inner, nfreq)
-    tables = [jnp.asarray(t, dtype=BF16) for t in (forward, inverse, gather, scatter)]
+    tables = [jnp.asarray(t, dtype=BF16) for t in (forward, inverse)]
     hbm = pl.BlockSpec(memory_space=pl.ANY)
     dma = pltpu.SemaphoreType.DMA
 
@@ -415,7 +409,7 @@
     fields = pl.pallas_call(
         functools.partial(kernel, ny, nz, npts),
         out_shape=jax.ShapeDtypeStruct((2, nt, cells), F32),
-        in_specs=[hbm] * 9,
+        in_specs=[hbm] * 7,
         out_specs=pl.BlockSpec(memory_space=pltpu.VMEM),
         scratch_shapes=[
             pltpu.VMEM((nt, cells), BF16),
@@ -431,7 +425,7 @@
             pltpu.VMEM((tiles, pairs, nfreq, inner, NB), BF16),
             pltpu.VMEM((pairs, tiles, ntl, K, inner * nfreq), BF16),
             pltpu.VMEM((2, pairs, ntl, tiles, K, inner * nfreq), BF16),
-            dma((8,)),
+            dma((6,)),
             dma,
             dma((pairs, tiles)),
             dma((tiles,)),

time: 175 us -> 174 us (level)
  no operation moved by 1% of the time
where the time goes in v3:
time: 174 us
  Pallas kernels  172 us (99%)
  local copies, waits for them, and re-layouts  1.86 us (1%)
    pallas_call x1, Pallas kernels, body(): pl.pallas_call(functools.partial(kernel, ny, nz, npts), out_shape=jax.Sha...  172 us

profile of v3, /device:TPU:1, one launch (start us, length us, event | category | flops | bytes accessed | tf_op | source)
XLA Modules:
  0.0 174.1 jit_solution(7077404331190526782)
XLA Ops:
  0.6 171.6 %shard_map.86 = f32[2,512,768]{2,1,0:T(8,128)S(1)} custom-call(bf16[1,512,768]{2,1,0:T(8,128)(2,1)} %direct_hbm.1, s32[1,768]{1,0:T(1,128)} %onsets_hbm.1, bf16[4,3,24,2,8,256]{5,4,3,2,1,0:T(8,128)(2,1)} %left_ref.1, bf16[4,3,24,2,8,256]{5,4,3,2,1,0:T(8,128)(2,1)} %right_ref.1, s32[3,4,24]{2,1,0:T(4,128)} %bitcast.1, ...), custom_call_target="tpu_custom_call" | custom-call | tf_op jit(solution)/shard_map/pallas_call | solution.py:409
  172.3 1.9 %fusion = (f32[1,512,768]{2,1,0:T(8,128)}, f32[1,512,768]{2,1,0:T(8,128)}) fusion(f32[2,512,768]{2,1,0:T(8,128)S(1)} %shard_map.86), kind=kLoop, calls=%fused_computation | loop fusion | bytes 6291456 | tf_op jit(solution)/shard_map/slice | solution.py:449
